TPU v7x, 32 devices: a whole 2x2x4 slice. The times are simulated.
32 devices in a mesh: parts: 2 (over y), gz: 8 (over z, x), gy: 2 (over core).
Axes of the slice: x: 2, y: 2, z: 4, core: 2. Of those that a mesh axis runs over, the one named last changes fastest.
Arguments:
- direction: float32 [3, 16, 128, 128], P(None, ('parts', 'gz'), 'gy'), parts along dimension 1, may hold values from -6 to 6
- region: int32 [16, 128, 128], P(('parts', 'gz'), 'gy'), parts along dimension 0, may hold values from 0 to 3
- saturation: float32 [3], replicated, may hold values from 0.5 to 2
- kernel_main: float32 [6, 16, 256, 128], P(None, 'gz', 'gy'), may hold values from -6 to 6
- kernel_nyq: float32 [6, 16, 256], P(None, 'gz', 'gy'), may hold values from -6 to 6
Outputs:
- field: float32 [3, 16, 128, 128], P(None, ('parts', 'gz'), 'gy'), parts along dimension 1
There are 2 independent parts, one for each index of `parts`. A program takes and returns all parts, laid end to end along the dimension named above; an argument that names none is the same for every part. Nothing has to cross between parts.
Inputs may be any that keep to these rules, and one draw needn't show every extreme that they name: `region`: 0 marks an empty cell; other ids name materials.
All inputs are finite; a program needn't handle non-finite values.
Results may differ from a plain program's by a relative error of at most 0.00007.
Values sent between devices are 32-bit elements; how exact they have to be, the bound alone decides.
A program may use at most 64 MiB of HBM per device.

v0:
```python
import math
import jax
import jax.numpy as jnp
from jax import lax
from jax.sharding import PartitionSpec as P

exchange_stiffness = 0.25
tensor_index = ((0, 3, 4), (3, 1, 5), (4, 5, 2))
highest = lax.Precision.HIGHEST


def with_halo(cells, sides, width):
    for axis, dim in sides:
        count = lax.axis_size(axis)
        ends = count - 1
        head = lax.slice_in_dim(cells, 0, width, axis=dim)
        tail = lax.slice_in_dim(cells, cells.shape[dim] - width, cells.shape[dim], axis=dim)
        cells = jnp.concatenate(
            [
                lax.ppermute(tail, axis, [(i, (i + 1) % count) for i in range(ends)]),
                cells,
                lax.ppermute(head, axis, [((i + 1) % count, i) for i in range(ends)]),
            ],
            axis=dim,
        )
    return cells


def phase(first, second, period):
    product = first[:, None] * second[None, :] % period
    angle = 2.0 * math.pi / period * product.astype(jnp.float32)
    return (jnp.cos(angle), jnp.sin(angle))


def slot_frequency(slot_index, bit_count):
    device = slot_index // 2
    reversed_bits = jnp.zeros_like(device)
    for b in range(bit_count):
        reversed_bits = reversed_bits + device // 2**b % 2 * 2 ** (bit_count - 1 - b)
    return 2 * reversed_bits + slot_index % 2


def row_transform(plane):
    columns = plane.shape[2]
    row_count = plane.shape[1]
    positions = jnp.arange(columns, dtype=jnp.int32)
    cosine, sine = phase(positions, positions, 2 * columns)
    table = jnp.concatenate([cosine, -sine], axis=1)
    flat = plane.reshape(3 * row_count, columns)
    both = jnp.dot(flat, table, precision=highest).reshape(3, row_count, 2, columns)
    signs = 1.0 - 2.0 * (positions % 2).astype(jnp.float32)
    nyquist = jnp.dot(flat, signs, precision=highest).reshape(3, row_count)
    return (both[:, :, 0], both[:, :, 1], nyquist)


def column_transform(real_rows, imag_rows, nyquist, cosine, sine):
    new_real = jnp.einsum("kr,crx->ckx", cosine, real_rows, precision=highest) + jnp.einsum(
        "kr,crx->ckx", sine, imag_rows, precision=highest
    )
    new_imag = jnp.einsum("kr,crx->ckx", cosine, imag_rows, precision=highest) - jnp.einsum(
        "kr,crx->ckx", sine, real_rows, precision=highest
    )
    nyq_real = jnp.einsum("kr,cr->ck", cosine, nyquist, precision=highest)
    nyq_imag = -jnp.einsum("kr,cr->ck", sine, nyquist, precision=highest)
    return (jnp.stack([new_real, new_imag], axis=1), jnp.stack([nyq_real, nyq_imag], axis=1))


def plane_transform(values, cosine, sine, direction_sign):
    real_part = values[:, 0]
    imag_part = values[:, 1]
    new_real = jnp.einsum(
        "pz,cz...->cp...", cosine, real_part, precision=highest
    ) - direction_sign * jnp.einsum("pz,cz...->cp...", sine, imag_part, precision=highest)
    new_imag = jnp.einsum(
        "pz,cz...->cp...", cosine, imag_part, precision=highest
    ) + direction_sign * jnp.einsum("pz,cz...->cp...", sine, real_part, precision=highest)
    return jnp.stack([new_real, new_imag], axis=1)


def apply_kernel(spectra, kernel):
    pieces = []
    for i in range(3):
        summed = kernel[tensor_index[i][0]] * spectra[0]
        for j in (1, 2):
            summed = summed + kernel[tensor_index[i][j]] * spectra[j]
        pieces.append(summed)
    return jnp.stack(pieces)


def local(direction, region, saturation, kernel_main, kernel_nyq):
    columns = direction.shape[3]
    own_rows = direction.shape[2]
    groups_y = lax.axis_size("gy")
    groups_z = lax.axis_size("gz")
    bit_count = groups_z.bit_length() - 1
    rows_total = own_rows * groups_y
    period_y = 2 * rows_total
    period_z = 2 * groups_z
    period_x = 2 * columns
    spec_rows = period_y // groups_y
    y_index = lax.axis_index("gy")
    magnetic = (region > 0).astype(jnp.float32)
    strength = jnp.zeros(region.shape, jnp.float32)
    for r in range(saturation.shape[0]):
        strength = strength + jnp.where(region == r + 1, saturation[r], 0.0)
    magnet_plane = (direction * strength[None])[:, 0]
    gathered = lax.all_gather(magnet_plane, "gy", axis=1, tiled=True)
    frequency = y_index * spec_rows + jnp.arange(spec_rows, dtype=jnp.int32)
    cosine, sine = phase(frequency, jnp.arange(rows_total, dtype=jnp.int32), period_y)
    real_rows, imag_rows, nyquist = row_transform(gathered)
    spec_main, spec_nyq = column_transform(real_rows, imag_rows, nyquist, cosine, sine)
    slot_freq = slot_frequency(jnp.arange(period_z, dtype=jnp.int32), bit_count)
    plane_ids = jnp.arange(groups_z, dtype=jnp.int32)
    sent_main, sent_nyq = (
        lax.all_to_all(spec_main[:, :, None], "gz", split_axis=3, concat_axis=2, tiled=True),
        lax.all_to_all(spec_nyq[:, :, None], "gz", split_axis=3, concat_axis=2, tiled=True),
    )
    cosine, sine = phase(slot_freq, plane_ids, period_z)
    done_main = plane_transform(sent_main, cosine, sine, -1.0)
    done_nyq = plane_transform(sent_nyq, cosine, sine, -1.0)
    full_main, full_nyq = (
        lax.all_to_all(done_main, "gz", split_axis=2, concat_axis=3, tiled=True),
        lax.all_to_all(done_nyq, "gz", split_axis=2, concat_axis=3, tiled=True),
    )
    field_main = apply_kernel(full_main, kernel_main)
    field_nyq = apply_kernel(full_nyq, kernel_nyq)
    out_main, out_nyq = (
        lax.all_to_all(field_main, "gz", split_axis=3, concat_axis=2, tiled=True),
        lax.all_to_all(field_nyq, "gz", split_axis=3, concat_axis=2, tiled=True),
    )
    cosine, sine = phase(plane_ids, slot_freq, period_z)
    back_main = plane_transform(out_main, cosine, sine, 1.0)
    back_nyq = plane_transform(out_nyq, cosine, sine, 1.0)
    plane_main, plane_nyq = (
        lax.all_to_all(back_main, "gz", split_axis=2, concat_axis=3, tiled=True),
        lax.all_to_all(back_nyq, "gz", split_axis=2, concat_axis=3, tiled=True),
    )
    plane_main = plane_main[:, :, 0]
    plane_nyq = plane_nyq[:, :, 0]
    frequency = y_index * spec_rows + jnp.arange(spec_rows, dtype=jnp.int32)
    cosine, sine = phase(jnp.arange(rows_total, dtype=jnp.int32), frequency, period_y)
    term_real = jnp.einsum("yk,ckx->cyx", cosine, plane_main[:, 0], precision=highest) - jnp.einsum(
        "yk,ckx->cyx", sine, plane_main[:, 1], precision=highest
    )
    term_imag = jnp.einsum("yk,ckx->cyx", cosine, plane_main[:, 1], precision=highest) + jnp.einsum(
        "yk,ckx->cyx", sine, plane_main[:, 0], precision=highest
    )
    nyq_real = jnp.einsum("yk,ck->cy", cosine, plane_nyq[:, 0], precision=highest) - jnp.einsum(
        "yk,ck->cy", sine, plane_nyq[:, 1], precision=highest
    )
    nyq_imag = jnp.einsum("yk,ck->cy", cosine, plane_nyq[:, 1], precision=highest) + jnp.einsum(
        "yk,ck->cy", sine, plane_nyq[:, 0], precision=highest
    )
    rows_main, rows_nyq = (
        lax.psum_scatter(
            jnp.stack([term_real, term_imag], axis=1), "gy", scatter_dimension=2, tiled=True
        ),
        lax.psum_scatter(
            jnp.stack([nyq_real, nyq_imag], axis=1), "gy", scatter_dimension=2, tiled=True
        ),
    )
    positions = jnp.arange(columns, dtype=jnp.int32)
    cosine, sine = phase(positions, positions, period_x)
    weights = jnp.where(positions == 0, 1.0, 2.0).astype(jnp.float32)[:, None]
    table = jnp.concatenate([weights * cosine, -weights * sine], axis=0)
    flat = jnp.concatenate([rows_main[:, 0], rows_main[:, 1]], axis=2).reshape(
        3 * own_rows, 2 * columns
    )
    signs = 1.0 - 2.0 * (positions % 2).astype(jnp.float32)
    demag = jnp.dot(flat, table, precision=highest).reshape(3, own_rows, columns)
    demag = demag + rows_nyq[:, 0][:, :, None] * signs[None, None, :]
    demag = demag * (1.0 / (period_x * period_y * period_z))
    moment = direction * magnetic[None]
    stacked = jnp.concatenate([moment, magnetic[None]], axis=0)
    rim = with_halo(stacked, (("gz", 1), ("gy", 2)), 1)
    centre = rim[:, 1:2, 1:-1]
    near = rim[:, 0:1, 1:-1] + rim[:, 2:3, 1:-1] + rim[:, 1:2, :-2] + rim[:, 1:2, 2:]
    padded_x = jnp.pad(centre, ((0, 0), (0, 0), (0, 0), (1, 1)))
    near = near + padded_x[..., :-2] + padded_x[..., 2:]
    exchange = exchange_stiffness * magnetic[None] * (near[:3] - near[3:4] * direction)
    return demag[:, None] + exchange


def solution(mesh):
    placed = (
        P(None, ("parts", "gz"), "gy", None),
        P(("parts", "gz"), "gy", None),
        P(),
        P(None, "gz", "gy", None),
        P(None, "gz", "gy"),
    )
    return jax.shard_map(
        local,
        mesh=mesh,
        in_specs=placed,
        out_specs=P(None, ("parts", "gz"), "gy", None),
        check_vma=False,
    )
```

profile of v0, /device:TPU:0, one launch (start us, length us, event | category | flops | bytes accessed | tf_op | source)
XLA Modules:
  0.0 176.9 jit_solution(13148347249901439266)
XLA Ops:
  9.4 1.9 %add_bitcast_fusion = f32[64,128]{1,0:T(8,128)S(1)} fusion(s32[1,64,128]{2,1,0:T(8,128)S(1)} %copy-done.2, f32[]{:T(128)} %bitcast.4, f32[]{:T(128)} %bitcast.3, f32[]{:T(128)} %bitcast.2), kind=kLoop, calls=%fused_computation.163 | loop fusion | flops 65536 | bytes 65548 | tf_op jit(solution)/shard_map/mul | solution.py:106
  11.3 2.1 %all-gather = f32[3,1,128,128]{3,2,0,1:T(8,128)S(1)} all-gather(f32[3,1,64,128]{3,2,0,1:T(8,128)S(1)} %get-tuple-element.28), channel_id=2, replica_groups=mesh['parts'=2,'gz'=8,'gy'=2] {'gy'}, dimensions={2}, use_global_device_ids=true | all-gather | bytes 294912 | tf_op jit(solution)/shard_map/all_gather | solution.py:107
  14.8 0.8 copy.150
  15.6 7.1 %all-to-all-start.4 = ((f32[3,2,1,128]{0,1,2,3:T(2,128)}), f32[3,2,1,128]{0,1,2,3:T(2,128)S(1)}, u32[]{:S(2)}, u32[]{:S(2)}) async-start(f32[3,2,1,128]{0,1,2,3:T(2,128)} %copy.150), calls=%async_computation.4 | async-start | bytes 262144 | tf_op jit(solution)/shard_map/all_to_all | solution.py:116
  26.4 3.7 %all-to-all-done.4 = f32[3,2,1,128]{0,1,2,3:T(2,128)S(1)} async-done(((f32[3,2,1,128]{0,1,2,3:T(2,128)}), f32[3,2,1,128]{0,1,2,3:T(2,128)S(1)}, u32[]{:S(2)}, u32[]{:S(2)}) %all-to-all-start.4) | async-done | bytes 3104 | tf_op jit(solution)/shard_map/all_to_all | solution.py:116
  32.2 3.3 %all-to-all-start.5 = ((f32[8,1,192]{2,1,0:T(1,128)}), f32[8,1,192]{2,1,0:T(1,128)S(1)}, u32[]{:S(2)}, u32[]{:S(2)}) async-start(f32[8,1,192]{2,1,0:T(1,128)} %reshape.497), calls=%async_computation.5 | async-start | bytes 16384 | tf_op jit(solution)/shard_map/all_to_all | solution.py:123
  35.6 0.9 copy.131
  36.5 5.5 %all-to-all-done.5 = f32[8,1,192]{2,1,0:T(1,128)S(1)} async-done(((f32[8,1,192]{2,1,0:T(1,128)}), f32[8,1,192]{2,1,0:T(1,128)S(1)}, u32[]{:S(2)}, u32[]{:S(2)}) %all-to-all-start.5) | async-done | bytes 6176 | tf_op jit(solution)/shard_map/all_to_all | solution.py:123
  42.0 3.5 %all-to-all-start = ((f32[3,2,1,128,128]{4,1,2,0,3:T(2,128)}), f32[3,2,1,128,128]{4,1,2,0,3:T(2,128)S(1)}, u32[]{:S(2)}, u32[]{:S(2)}) async-start(f32[3,2,1,128,128]{4,1,2,0,3:T(2,128)} %copy.131), calls=%async_computation | async-start | bytes 786432 | tf_op jit(solution)/shard_map/all_to_all | solution.py:115
  47.2 1.0 reshape.499
  48.2 7.0 %all-to-all-done = f32[3,2,1,128,128]{4,1,2,0,3:T(2,128)S(1)} async-done(((f32[3,2,1,128,128]{4,1,2,0,3:T(2,128)}), f32[3,2,1,128,128]{4,1,2,0,3:T(2,128)S(1)}, u32[]{:S(2)}, u32[]{:S(2)}) %all-to-all-start) | async-done | bytes 393248 | tf_op jit(solution)/shard_map/all_to_all | solution.py:115
  55.2 3.7 %all-to-all-start.6 = ((f32[8,1,192]{2,1,0:T(1,128)}), f32[8,1,192]{2,1,0:T(1,128)S(1)}, u32[]{:S(2)}, u32[]{:S(2)}) async-start(f32[8,1,192]{2,1,0:T(1,128)} %reshape.499), calls=%async_computation.6 | async-start | bytes 16384 | tf_op jit(solution)/shard_map/all_to_all | solution.py:129
  61.3 1.1 copy.135
  62.4 2.9 %all-to-all-done.6 = f32[8,1,192]{2,1,0:T(1,128)S(1)} async-done(((f32[8,1,192]{2,1,0:T(1,128)}), f32[8,1,192]{2,1,0:T(1,128)S(1)}, u32[]{:S(2)}, u32[]{:S(2)}) %all-to-all-start.6) | async-done | bytes 6176 | tf_op jit(solution)/shard_map/all_to_all | solution.py:129
  65.4 3.5 %all-to-all-start.1 = ((f32[3,2,16,16,128]{4,3,0,1,2:T(8,128)}), f32[3,2,16,16,128]{4,3,0,1,2:T(8,128)S(1)}, u32[]{:S(2)}, u32[]{:S(2)}) async-start(f32[3,2,16,16,128]{4,3,0,1,2:T(8,128)} %copy.135), calls=%async_computation.1 | async-start | bytes 1572864 | tf_op jit(solution)/shard_map/all_to_all | solution.py:122
  71.7 15.7 %all-to-all-done.1 = f32[3,2,16,16,128]{4,3,0,1,2:T(8,128)S(1)} async-done(((f32[3,2,16,16,128]{4,3,0,1,2:T(8,128)}), f32[3,2,16,16,128]{4,3,0,1,2:T(8,128)S(1)}, u32[]{:S(2)}, u32[]{:S(2)}) %all-to-all-start.1) | async-done | bytes 786464 | tf_op jit(solution)/shard_map/all_to_all | solution.py:122
  87.4 3.5 %all-to-all-start.7 = ((f32[3,2,8,16]{3,1,0,2:T(2,128)}), f32[3,2,8,16]{3,1,0,2:T(2,128)S(1)}, u32[]{:S(2)}, u32[]{:S(2)}) async-start(f32[3,2,8,16]{3,1,0,2:T(2,128)} %copy.162), calls=%async_computation.7 | async-start | bytes 49152 | tf_op jit(solution)/shard_map/all_to_all | solution.py:136
  91.4 1.5 copy.140
  92.9 4.7 %all-to-all-done.7 = f32[3,2,8,16]{3,1,0,2:T(2,128)S(1)} async-done(((f32[3,2,8,16]{3,1,0,2:T(2,128)}), f32[3,2,8,16]{3,1,0,2:T(2,128)S(1)}, u32[]{:S(2)}, u32[]{:S(2)}) %all-to-all-start.7) | async-done | bytes 3104 | tf_op jit(solution)/shard_map/all_to_all | solution.py:136
  97.6 3.5 %all-to-all-start.2 = ((f32[3,2,2,128,128]{4,2,1,0,3:T(2,128)}), f32[3,2,2,128,128]{4,2,1,0,3:T(2,128)S(1)}, u32[]{:S(2)}, u32[]{:S(2)}) async-start(f32[3,2,2,128,128]{4,2,1,0,3:T(2,128)} %copy.140), calls=%async_computation.2 | async-start | bytes 1572864 | tf_op jit(solution)/shard_map/all_to_all | solution.py:128
  101.1 3.8 %collective-permute-start = (f32[4,1,64,128]{3,2,0,1:T(8,128)S(1)}, f32[4,1,64,128]{3,2,0,1:T(8,128)S(1)}, u32[]{:S(2)}, u32[]{:S(2)}) collective-permute-start(f32[4,1,64,128]{3,2,0,1:T(8,128)S(1)} %pad_maximum_fusion.12), channel_id=1, source_target_pairs={{0,2},{2,4},{4,6},{6,8},{8,10},{10,12},{12,14},{1,3},{3,5},{5,7},{... | collective-permute-start | bytes 393224 | tf_op jit(solution)/shard_map/ppermute | solution.py:20
  105.0 1.5 collective-permute-start.1
  107.3 13.6 %all-to-all-done.2 = f32[3,2,2,128,128]{4,2,1,0,3:T(2,128)S(1)} async-done(((f32[3,2,2,128,128]{4,2,1,0,3:T(2,128)}), f32[3,2,2,128,128]{4,2,1,0,3:T(2,128)S(1)}, u32[]{:S(2)}, u32[]{:S(2)}) %all-to-all-start.2) | async-done | bytes 786464 | tf_op jit(solution)/shard_map/all_to_all | solution.py:128
  123.9 3.5 %all-to-all-start.3 = ((f32[3,2,8,16,128]{4,3,0,1,2:T(8,128)}), f32[3,2,8,16,128]{4,3,0,1,2:T(8,128)S(1)}, u32[]{:S(2)}, u32[]{:S(2)}) async-start(f32[3,2,8,16,128]{4,3,0,1,2:T(8,128)} %copy.143), calls=%async_computation.3 | async-start | bytes 786432 | tf_op jit(solution)/shard_map/all_to_all | solution.py:135
  131.8 7.5 %reduce-scatter.4.cloned.1.call-done = f32[64,6]{1,0:T(8,128)} async-done(((f32[128,6]{1,0:T(8,128)}), f32[64,6]{1,0:T(8,128)}) %reduce-scatter.4.cloned.1.call-update) | async-done | bytes 1552
  139.2 0.9 reshape.495
  140.2 2.1 %collective-permute-start.2 = (f32[4,3,1,128]{3,2,0,1:T(1,128)S(1)}, f32[4,3,1,128]{3,2,0,1:T(1,128)S(1)}, u32[]{:S(2)}, u32[]{:S(2)}) collective-permute-start(f32[4,3,1,128]{3,2,0,1:T(1,128)S(1)} %get-tuple-element.19), channel_id=1, source_target_pairs={{0,1},{2,3},{4,5},{6,7},{8,9},{10,11},{12,13},{14,15},{16,17},{18,... | collective-permute-start | bytes 18440 | tf_op jit(solution)/shard_map/ppermute | solution.py:20
  142.3 1.3 collective-permute-start.3
  146.3 0.9 copy.147
  147.5 20.4 %all-reduce.4.cloned.1.call-done = f32[3,2,128,128]{3,1,0,2:T(2,128)} async-done(((f32[3,2,128,128]{3,1,0,2:T(2,128)}), f32[3,2,128,128]{3,1,0,2:T(2,128)}) %all-reduce.4.cloned.1.call-update) | async-done | bytes 393232
  167.9 1.2 constant_dynamic-slice_fusion
  169.1 1.0 fusion.11
  (127 shorter events, 27.5 us)
Async XLA Ops:
  6.5 0.7 copy-start.4
  7.8 3.5 %copy-start.1 = (f32[3,1,64,128]{3,2,1,0:T(8,128)S(1)}, f32[3,1,64,128]{3,2,1,0:T(8,128)}, u32[]{:S(2)}) copy-start(f32[3,1,64,128]{3,2,1,0:T(8,128)} %param.5) | copy-start | bytes 294916
  8.6 0.8 copy-start.2
  15.6 14.5 %all-to-all-start.4 = ((f32[3,2,1,128]{0,1,2,3:T(2,128)}), f32[3,2,1,128]{0,1,2,3:T(2,128)S(1)}, u32[]{:S(2)}, u32[]{:S(2)}) async-start(f32[3,2,1,128]{0,1,2,3:T(2,128)} %copy.150), calls=%async_computation.4 | async-start | bytes 262144 | tf_op jit(solution)/shard_map/all_to_all | solution.py:116
  32.2 9.8 %all-to-all-start.5 = ((f32[8,1,192]{2,1,0:T(1,128)}), f32[8,1,192]{2,1,0:T(1,128)S(1)}, u32[]{:S(2)}, u32[]{:S(2)}) async-start(f32[8,1,192]{2,1,0:T(1,128)} %reshape.497), calls=%async_computation.5 | async-start | bytes 16384 | tf_op jit(solution)/shard_map/all_to_all | solution.py:123
  36.5 9.0 %copy-start.3 = (f32[6,2,128]{2,1,0:T(2,128)S(1)}, f32[6,2,128]{2,1,0:T(2,128)}, u32[]{:S(2)}) copy-start(f32[6,2,128]{2,1,0:T(2,128)} %param.9) | copy-start | bytes 18436
  42.0 13.2 %all-to-all-start = ((f32[3,2,1,128,128]{4,1,2,0,3:T(2,128)}), f32[3,2,1,128,128]{4,1,2,0,3:T(2,128)S(1)}, u32[]{:S(2)}, u32[]{:S(2)}) async-start(f32[3,2,1,128,128]{4,1,2,0,3:T(2,128)} %copy.131), calls=%async_computation | async-start | bytes 786432 | tf_op jit(solution)/shard_map/all_to_all | solution.py:115
  55.2 10.2 %all-to-all-start.6 = ((f32[8,1,192]{2,1,0:T(1,128)}), f32[8,1,192]{2,1,0:T(1,128)S(1)}, u32[]{:S(2)}, u32[]{:S(2)}) async-start(f32[8,1,192]{2,1,0:T(1,128)} %reshape.499), calls=%async_computation.6 | async-start | bytes 16384 | tf_op jit(solution)/shard_map/all_to_all | solution.py:129
  62.4 6.5 %copy-start = (f32[6,2,128,128]{3,2,1,0:T(8,128)S(1)}, f32[6,2,128,128]{3,2,1,0:T(8,128)}, u32[]{:S(2)}) copy-start(f32[6,2,128,128]{3,2,1,0:T(8,128)} %param.8) | copy-start | bytes 2359300
  65.4 22.0 %all-to-all-start.1 = ((f32[3,2,16,16,128]{4,3,0,1,2:T(8,128)}), f32[3,2,16,16,128]{4,3,0,1,2:T(8,128)S(1)}, u32[]{:S(2)}, u32[]{:S(2)}) async-start(f32[3,2,16,16,128]{4,3,0,1,2:T(8,128)} %copy.135), calls=%async_computation.1 | async-start | bytes 1572864 | tf_op jit(solution)/shard_map/all_to_all | solution.py:122
  87.4 10.2 %all-to-all-start.7 = ((f32[3,2,8,16]{3,1,0,2:T(2,128)}), f32[3,2,8,16]{3,1,0,2:T(2,128)S(1)}, u32[]{:S(2)}, u32[]{:S(2)}) async-start(f32[3,2,8,16]{3,1,0,2:T(2,128)} %copy.162), calls=%async_computation.7 | async-start | bytes 49152 | tf_op jit(solution)/shard_map/all_to_all | solution.py:136
  97.6 23.3 %all-to-all-start.2 = ((f32[3,2,2,128,128]{4,2,1,0,3:T(2,128)}), f32[3,2,2,128,128]{4,2,1,0,3:T(2,128)S(1)}, u32[]{:S(2)}, u32[]{:S(2)}) async-start(f32[3,2,2,128,128]{4,2,1,0,3:T(2,128)} %copy.140), calls=%async_computation.2 | async-start | bytes 1572864 | tf_op jit(solution)/shard_map/all_to_all | solution.py:128
  101.1 39.1 %collective-permute-start = (f32[4,1,64,128]{3,2,0,1:T(8,128)S(1)}, f32[4,1,64,128]{3,2,0,1:T(8,128)S(1)}, u32[]{:S(2)}, u32[]{:S(2)}) collective-permute-start(f32[4,1,64,128]{3,2,0,1:T(8,128)S(1)} %pad_maximum_fusion.12), channel_id=1, source_target_pairs={{0,2},{2,4},{4,6},{6,8},{8,10},{10,12},{12,14},{1,3},{3,5},{5,7},{... | collective-permute-start | bytes 393224 | tf_op jit(solution)/shard_map/ppermute | solution.py:20
  105.0 35.2 %collective-permute-start.1 = (f32[4,1,64,128]{3,2,0,1:T(8,128)S(1)}, f32[4,1,64,128]{3,2,0,1:T(8,128)S(1)}, u32[]{:S(2)}, u32[]{:S(2)}) collective-permute-start(f32[4,1,64,128]{3,2,0,1:T(8,128)S(1)} %pad_maximum_fusion.12), channel_id=1, source_target_pairs={{2,0},{4,2},{6,4},{8,6},{10,8},{12,10},{14,12},{3,1},{5,3},{7,5},{... | collective-permute-start | bytes 393224 | tf_op jit(solution)/shard_map/ppermute | solution.py:22
  123.9 19.8 %all-to-all-start.3 = ((f32[3,2,8,16,128]{4,3,0,1,2:T(8,128)}), f32[3,2,8,16,128]{4,3,0,1,2:T(8,128)S(1)}, u32[]{:S(2)}, u32[]{:S(2)}) async-start(f32[3,2,8,16,128]{4,3,0,1,2:T(8,128)} %copy.143), calls=%async_computation.3 | async-start | bytes 786432 | tf_op jit(solution)/shard_map/all_to_all | solution.py:135
  127.3 11.9 %reduce-scatter.4.cloned.1.call-start = ((), (), s32[]{:S(2)}) async-start(), calls=%async_computation.9 | async-start | bytes 98304
  129.7 38.2 %all-reduce.4.cloned.1.call-start = ((), (), s32[]{:S(2)}) async-start(), calls=%async_computation.10 | async-start | bytes 786432
  129.8 0.7 copy-start.5
  140.2 7.1 %collective-permute-start.2 = (f32[4,3,1,128]{3,2,0,1:T(1,128)S(1)}, f32[4,3,1,128]{3,2,0,1:T(1,128)S(1)}, u32[]{:S(2)}, u32[]{:S(2)}) collective-permute-start(f32[4,3,1,128]{3,2,0,1:T(1,128)S(1)} %get-tuple-element.19), channel_id=1, source_target_pairs={{0,1},{2,3},{4,5},{6,7},{8,9},{10,11},{12,13},{14,15},{16,17},{18,... | collective-permute-start | bytes 18440 | tf_op jit(solution)/shard_map/ppermute | solution.py:20
  142.3 4.9 %collective-permute-start.3 = (f32[4,3,1,128]{3,2,0,1:T(1,128)S(1)}, f32[4,3,1,128]{3,2,0,1:T(1,128)S(1)}, u32[]{:S(2)}, u32[]{:S(2)}) collective-permute-start(f32[4,3,1,128]{3,2,0,1:T(1,128)S(1)} %get-tuple-element.20), channel_id=1, source_target_pairs={{1,0},{3,2},{5,4},{7,6},{9,8},{11,10},{13,12},{15,14},{17,16},{19,... | collective-permute-start | bytes 18440 | tf_op jit(solution)/shard_map/ppermute | solution.py:22
Sparse Core Ops, SparseCore 0:
  130.3 8.8 reduce-scatter.3
  147.4 20.4 all-reduce.3
where the time goes:
time: 178 us; the launch traced here: 177 us
  waiting for transfers between devices  81 us (46%)
  starting transfers between devices  40.5 us (23%)
  local copies, waits for them, and re-layouts  18.3 us (10%)
  matrix products  15.2 us (9%)
  between operations  14.8 us (8%)
  other arithmetic  5.07 us (3%)
  blocking collectives  2.08 us (1%)
    unnamed x4, waiting for transfers between devices  27.9 us
    all_to_all x1, waiting for transfers between devices, local(): lax.all_to_all(done_main, 'gz', split_axis=2, concat_axis=3, tiled=True)  15.7 us
    all_to_all x1, waiting for transfers between devices, local(): lax.all_to_all(field_main, 'gz', split_axis=3, concat_axis=2, tiled=True)  13.6 us
    all_to_all x1, starting transfers between devices, local(): lax.all_to_all(spec_nyq[:, :, None], 'gz', split_axis=3, concat_axis=2, t...  7.15 us
    all_to_all x1, waiting for transfers between devices, local(): lax.all_to_all(spec_main[:, :, None], 'gz', split_axis=3, concat_axis=2,...  7.02 us
    unnamed x25, local copies, waits for them, and re-layouts  6.98 us
    ppermute x2, starting transfers between devices, with_halo(): lax.ppermute(tail, axis, [(i, (i + 1) % count) for i in range(ends)])  5.94 us
    all_to_all x1, waiting for transfers between devices, local(): lax.all_to_all(done_nyq, 'gz', split_axis=2, concat_axis=3, tiled=True)  5.5 us
  transfers between devices with their start and end apart: 14, of which 9 were waited for; matrix products, arithmetic and copies ran while one was open for 15% of the time, Pallas kernels for 0%

commit v1 on v0

--- a/solution.py
+++ b/solution.py
@@ -7,6 +7,15 @@
 exchange_stiffness = 0.25
 tensor_index = ((0, 3, 4), (3, 1, 5), (4, 5, 2))
 highest = lax.Precision.HIGHEST
+fit_circles_all = lambda state, comm_axis: jnp.concatenate(
+    lax.all_to_all(
+        jnp.stack(jnp.split(state, lax.axis_size(comm_axis), axis=2), axis=0),
+        axis_name=comm_axis,
+        split_axis=0,
+        concat_axis=0,
+    ),
+    axis=3,
+)
 
 
 def with_halo(cells, sides, width):
@@ -119,7 +128,7 @@
     done_main = plane_transform(sent_main, cosine, sine, -1.0)
     done_nyq = plane_transform(sent_nyq, cosine, sine, -1.0)
     full_main, full_nyq = (
-        lax.all_to_all(done_main, "gz", split_axis=2, concat_axis=3, tiled=True),
+        fit_circles_all(done_main, "gz"),
         lax.all_to_all(done_nyq, "gz", split_axis=2, concat_axis=3, tiled=True),
     )
     field_main = apply_kernel(full_main, kernel_main)

time: 178 us -> 182 us (1.022)
  other arithmetic: 5.07 us -> 10.4 us
  starting transfers between devices: 40.5 us -> 43 us
  waiting for transfers between devices: 81 us -> 78.8 us
    unnamed x0 -> x7, other arithmetic: none -> 4.7 us
    all_to_all x1, waiting for transfers between devices: 2.94 us -> 0.01 us  [local(): lax.all_to_all(field_nyq, 'gz', split_axis=3, concat_axis=2, tiled=True)]
    all_to_all x1, starting transfers between devices: 3.55 us -> 6.13 us  [lax.all_to_all(jnp.stack(jnp.split(state, lax.axis_size(comm_axis), axis=...]
  transfers between devices with their start and end apart: 14 -> 14, of which waited for: 9 -> 8; matrix products, arithmetic and copies ran while one was open for 15% -> 17% of each run, Pallas kernels for 0% -> 0%
where the time goes in v1:
time: 182 us; the launch traced here: 181 us
  waiting for transfers between devices  78.8 us (43%)
  starting transfers between devices  43 us (24%)
  local copies, waits for them, and re-layouts  17.1 us (9%)
  matrix products  15.2 us (8%)
  between operations  14.8 us (8%)
  other arithmetic  10.4 us (6%)
  blocking collectives  2.08 us (1%)
    unnamed x4, waiting for transfers between devices  27.9 us
    all_to_all x1, waiting for transfers between devices, lax.all_to_all(jnp.stack(jnp.split(state, lax.axis_size(comm_axis), axis=...  16 us
    all_to_all x1, waiting for transfers between devices, local(): lax.all_to_all(field_main, 'gz', split_axis=3, concat_axis=2, tiled=True)  13.9 us
    all_to_all x1, starting transfers between devices, local(): lax.all_to_all(spec_nyq[:, :, None], 'gz', split_axis=3, concat_axis=2, t...  7.15 us
    all_to_all x1, waiting for transfers between devices, local(): lax.all_to_all(spec_main[:, :, None], 'gz', split_axis=3, concat_axis=2,...  7.02 us
    unnamed x25, local copies, waits for them, and re-layouts  6.99 us
    all_to_all x1, starting transfers between devices, lax.all_to_all(jnp.stack(jnp.split(state, lax.axis_size(comm_axis), axis=...  6.13 us
    ppermute x2, starting transfers between devices, with_halo(): lax.ppermute(tail, axis, [(i, (i + 1) % count) for i in range(ends)])  5.93 us
  transfers between devices with their start and end apart: 14, of which 8 were waited for; matrix products, arithmetic and copies ran while one was open for 17% of the time, Pallas kernels for 0%

profile of v1, /device:TPU:0, one launch (start us, length us, event | category | flops | bytes accessed | tf_op | source)
XLA Modules:
  0.0 181.4 jit_solution(17692676030102466235)
XLA Ops:
  7.8 0.8 broadcast_multiply_fusion.2
  9.4 1.9 %add_bitcast_fusion = f32[64,128]{1,0:T(8,128)S(1)} fusion(s32[1,64,128]{2,1,0:T(8,128)S(1)} %copy-done.2, f32[]{:T(128)} %bitcast.4, f32[]{:T(128)} %bitcast.3, f32[]{:T(128)} %bitcast.2), kind=kLoop, calls=%fused_computation.200 | loop fusion | flops 65536 | bytes 65548 | tf_op jit(solution)/shard_map/mul | solution.py:115
  11.3 2.1 %all-gather = f32[3,1,128,128]{3,2,0,1:T(8,128)S(1)} all-gather(f32[3,1,64,128]{3,2,0,1:T(8,128)S(1)} %get-tuple-element.28), channel_id=2, replica_groups=mesh['parts'=2,'gz'=8,'gy'=2] {'gy'}, dimensions={2}, use_global_device_ids=true | all-gather | bytes 294912 | tf_op jit(solution)/shard_map/all_gather | solution.py:116
  14.8 0.8 copy.110
  15.6 7.1 %all-to-all-start.4 = ((f32[3,2,1,128]{0,1,2,3:T(2,128)}), f32[3,2,1,128]{0,1,2,3:T(2,128)S(1)}, u32[]{:S(2)}, u32[]{:S(2)}) async-start(f32[3,2,1,128]{0,1,2,3:T(2,128)} %copy.110), calls=%async_computation.4 | async-start | bytes 262144 | tf_op jit(solution)/shard_map/all_to_all | solution.py:125
  26.4 3.7 %all-to-all-done.4 = f32[3,2,1,128]{0,1,2,3:T(2,128)S(1)} async-done(((f32[3,2,1,128]{0,1,2,3:T(2,128)}), f32[3,2,1,128]{0,1,2,3:T(2,128)S(1)}, u32[]{:S(2)}, u32[]{:S(2)}) %all-to-all-start.4) | async-done | bytes 3104 | tf_op jit(solution)/shard_map/all_to_all | solution.py:125
  32.2 3.3 %all-to-all-start.5 = ((f32[8,1,192]{2,1,0:T(1,128)}), f32[8,1,192]{2,1,0:T(1,128)S(1)}, u32[]{:S(2)}, u32[]{:S(2)}) async-start(f32[8,1,192]{2,1,0:T(1,128)} %reshape.502), calls=%async_computation.5 | async-start | bytes 16384 | tf_op jit(solution)/shard_map/all_to_all | solution.py:132
  35.6 0.9 copy.93
  36.5 5.5 %all-to-all-done.5 = f32[8,1,192]{2,1,0:T(1,128)S(1)} async-done(((f32[8,1,192]{2,1,0:T(1,128)}), f32[8,1,192]{2,1,0:T(1,128)S(1)}, u32[]{:S(2)}, u32[]{:S(2)}) %all-to-all-start.5) | async-done | bytes 6176 | tf_op jit(solution)/shard_map/all_to_all | solution.py:132
  42.0 3.5 %all-to-all-start = ((f32[3,2,1,128,128]{4,1,2,0,3:T(2,128)}), f32[3,2,1,128,128]{4,1,2,0,3:T(2,128)S(1)}, u32[]{:S(2)}, u32[]{:S(2)}) async-start(f32[3,2,1,128,128]{4,1,2,0,3:T(2,128)} %copy.93), calls=%async_computation | async-start | bytes 786432 | tf_op jit(solution)/shard_map/all_to_all | solution.py:124
  47.2 1.0 reshape.504
  48.2 7.0 %all-to-all-done = f32[3,2,1,128,128]{4,1,2,0,3:T(2,128)S(1)} async-done(((f32[3,2,1,128,128]{4,1,2,0,3:T(2,128)}), f32[3,2,1,128,128]{4,1,2,0,3:T(2,128)S(1)}, u32[]{:S(2)}, u32[]{:S(2)}) %all-to-all-start) | async-done | bytes 393248 | tf_op jit(solution)/shard_map/all_to_all | solution.py:124
  55.2 3.7 %all-to-all-start.6 = ((f32[8,1,192]{2,1,0:T(1,128)}), f32[8,1,192]{2,1,0:T(1,128)S(1)}, u32[]{:S(2)}, u32[]{:S(2)}) async-start(f32[8,1,192]{2,1,0:T(1,128)} %reshape.504), calls=%async_computation.6 | async-start | bytes 16384 | tf_op jit(solution)/shard_map/all_to_all | solution.py:138
  66.6 6.1 %all-to-all-start.1 = ((f32[8,3,2,2,16,128]{5,3,4,1,2,0:T(2,128)}), f32[8,3,2,2,16,128]{5,3,4,1,2,0:T(2,128)S(1)}, u32[]{:S(2)}, u32[]{:S(2)}) async-start(f32[8,3,2,2,16,128]{5,3,4,1,2,0:T(2,128)} %fusion.69), calls=%async_computation.1 | async-start | bytes 1572864 | tf_op jit(solution)/shard_map/all_to_all | solution.py:11
  75.5 16.0 %all-to-all-done.1 = f32[8,3,2,2,16,128]{5,3,4,1,2,0:T(2,128)S(1)} async-done(((f32[8,3,2,2,16,128]{5,3,4,1,2,0:T(2,128)}), f32[8,3,2,2,16,128]{5,3,4,1,2,0:T(2,128)S(1)}, u32[]{:S(2)}, u32[]{:S(2)}) %all-to-all-start.1) | async-done | bytes 786464 | tf_op jit(solution)/shard_map/all_to_all | solution.py:11
  91.6 3.5 %all-to-all-start.7 = ((f32[3,2,8,16]{3,1,0,2:T(2,128)}), f32[3,2,8,16]{3,1,0,2:T(2,128)S(1)}, u32[]{:S(2)}, u32[]{:S(2)}) async-start(f32[3,2,8,16]{3,1,0,2:T(2,128)} %copy.122), calls=%async_computation.7 | async-start | bytes 49152 | tf_op jit(solution)/shard_map/all_to_all | solution.py:145
  95.5 1.5 copy.100
  97.0 4.8 %all-to-all-done.7 = f32[3,2,8,16]{3,1,0,2:T(2,128)S(1)} async-done(((f32[3,2,8,16]{3,1,0,2:T(2,128)}), f32[3,2,8,16]{3,1,0,2:T(2,128)S(1)}, u32[]{:S(2)}, u32[]{:S(2)}) %all-to-all-start.7) | async-done | bytes 3104 | tf_op jit(solution)/shard_map/all_to_all | solution.py:145
  101.7 3.5 %all-to-all-start.2 = ((f32[3,2,2,128,128]{4,2,1,0,3:T(2,128)}), f32[3,2,2,128,128]{4,2,1,0,3:T(2,128)S(1)}, u32[]{:S(2)}, u32[]{:S(2)}) async-start(f32[3,2,2,128,128]{4,2,1,0,3:T(2,128)} %copy.100), calls=%async_computation.2 | async-start | bytes 1572864 | tf_op jit(solution)/shard_map/all_to_all | solution.py:137
  105.3 3.8 %collective-permute-start = (f32[4,1,64,128]{3,2,0,1:T(8,128)S(1)}, f32[4,1,64,128]{3,2,0,1:T(8,128)S(1)}, u32[]{:S(2)}, u32[]{:S(2)}) collective-permute-start(f32[4,1,64,128]{3,2,0,1:T(8,128)S(1)} %pad_maximum_fusion.11), channel_id=1, source_target_pairs={{0,2},{2,4},{4,6},{6,8},{8,10},{10,12},{12,14},{1,3},{3,5},{5,7},{... | collective-permute-start | bytes 393224 | tf_op jit(solution)/shard_map/ppermute | solution.py:29
  109.1 1.5 collective-permute-start.1
  111.4 13.9 %all-to-all-done.2 = f32[3,2,2,128,128]{4,2,1,0,3:T(2,128)S(1)} async-done(((f32[3,2,2,128,128]{4,2,1,0,3:T(2,128)}), f32[3,2,2,128,128]{4,2,1,0,3:T(2,128)S(1)}, u32[]{:S(2)}, u32[]{:S(2)}) %all-to-all-start.2) | async-done | bytes 786464 | tf_op jit(solution)/shard_map/all_to_all | solution.py:137
  127.5 0.8 copy.103
  128.3 3.5 %all-to-all-start.3 = ((f32[3,2,8,16,128]{4,3,0,1,2:T(8,128)}), f32[3,2,8,16,128]{4,3,0,1,2:T(8,128)S(1)}, u32[]{:S(2)}, u32[]{:S(2)}) async-start(f32[3,2,8,16,128]{4,3,0,1,2:T(8,128)} %copy.103), calls=%async_computation.3 | async-start | bytes 786432 | tf_op jit(solution)/shard_map/all_to_all | solution.py:144
  136.2 7.5 %reduce-scatter.4.cloned.1.call-done = f32[64,6]{1,0:T(8,128)} async-done(((f32[128,6]{1,0:T(8,128)}), f32[64,6]{1,0:T(8,128)}) %reduce-scatter.4.cloned.1.call-update) | async-done | bytes 1552
  143.7 0.9 reshape.500
  144.7 2.1 %collective-permute-start.2 = (f32[4,3,1,128]{3,2,0,1:T(1,128)S(1)}, f32[4,3,1,128]{3,2,0,1:T(1,128)S(1)}, u32[]{:S(2)}, u32[]{:S(2)}) collective-permute-start(f32[4,3,1,128]{3,2,0,1:T(1,128)S(1)} %get-tuple-element.19), channel_id=1, source_target_pairs={{0,1},{2,3},{4,5},{6,7},{8,9},{10,11},{12,13},{14,15},{16,17},{18,... | collective-permute-start | bytes 18440 | tf_op jit(solution)/shard_map/ppermute | solution.py:29
  146.8 1.3 collective-permute-start.3
  150.8 0.9 copy.107
  151.9 20.4 %all-reduce.4.cloned.1.call-done = f32[3,2,128,128]{3,1,0,2:T(2,128)} async-done(((f32[3,2,128,128]{3,1,0,2:T(2,128)}), f32[3,2,128,128]{3,1,0,2:T(2,128)}) %all-reduce.4.cloned.1.call-update) | async-done | bytes 393232
  172.3 1.2 constant_dynamic-slice_fusion
  173.6 1.0 fusion.11
  (132 shorter events, 31.1 us)
Async XLA Ops:
  6.5 0.7 copy-start.4
  7.8 3.5 %copy-start.1 = (f32[3,1,64,128]{3,2,1,0:T(8,128)S(1)}, f32[3,1,64,128]{3,2,1,0:T(8,128)}, u32[]{:S(2)}) copy-start(f32[3,1,64,128]{3,2,1,0:T(8,128)} %param.5) | copy-start | bytes 294916
  8.6 0.8 copy-start.2
  15.6 14.5 %all-to-all-start.4 = ((f32[3,2,1,128]{0,1,2,3:T(2,128)}), f32[3,2,1,128]{0,1,2,3:T(2,128)S(1)}, u32[]{:S(2)}, u32[]{:S(2)}) async-start(f32[3,2,1,128]{0,1,2,3:T(2,128)} %copy.110), calls=%async_computation.4 | async-start | bytes 262144 | tf_op jit(solution)/shard_map/all_to_all | solution.py:125
  32.2 9.8 %all-to-all-start.5 = ((f32[8,1,192]{2,1,0:T(1,128)}), f32[8,1,192]{2,1,0:T(1,128)S(1)}, u32[]{:S(2)}, u32[]{:S(2)}) async-start(f32[8,1,192]{2,1,0:T(1,128)} %reshape.502), calls=%async_computation.5 | async-start | bytes 16384 | tf_op jit(solution)/shard_map/all_to_all | solution.py:132
  36.5 9.0 %copy-start.3 = (f32[6,2,128]{2,1,0:T(2,128)S(1)}, f32[6,2,128]{2,1,0:T(2,128)}, u32[]{:S(2)}) copy-start(f32[6,2,128]{2,1,0:T(2,128)} %param.9) | copy-start | bytes 18436
  42.0 13.2 %all-to-all-start = ((f32[3,2,1,128,128]{4,1,2,0,3:T(2,128)}), f32[3,2,1,128,128]{4,1,2,0,3:T(2,128)S(1)}, u32[]{:S(2)}, u32[]{:S(2)}) async-start(f32[3,2,1,128,128]{4,1,2,0,3:T(2,128)} %copy.93), calls=%async_computation | async-start | bytes 786432 | tf_op jit(solution)/shard_map/all_to_all | solution.py:124
  55.2 11.4 %all-to-all-start.6 = ((f32[8,1,192]{2,1,0:T(1,128)}), f32[8,1,192]{2,1,0:T(1,128)S(1)}, u32[]{:S(2)}, u32[]{:S(2)}) async-start(f32[8,1,192]{2,1,0:T(1,128)} %reshape.504), calls=%async_computation.6 | async-start | bytes 16384 | tf_op jit(solution)/shard_map/all_to_all | solution.py:138
  66.6 6.1 %copy-start = (f32[6,2,128,128]{3,2,1,0:T(8,128)S(1)}, f32[6,2,128,128]{3,2,1,0:T(8,128)}, u32[]{:S(2)}) copy-start(f32[6,2,128,128]{3,2,1,0:T(8,128)} %param.8) | copy-start | bytes 2359300
  66.6 24.9 %all-to-all-start.1 = ((f32[8,3,2,2,16,128]{5,3,4,1,2,0:T(2,128)}), f32[8,3,2,2,16,128]{5,3,4,1,2,0:T(2,128)S(1)}, u32[]{:S(2)}, u32[]{:S(2)}) async-start(f32[8,3,2,2,16,128]{5,3,4,1,2,0:T(2,128)} %fusion.69), calls=%async_computation.1 | async-start | bytes 1572864 | tf_op jit(solution)/shard_map/all_to_all | solution.py:11
  91.6 10.2 %all-to-all-start.7 = ((f32[3,2,8,16]{3,1,0,2:T(2,128)}), f32[3,2,8,16]{3,1,0,2:T(2,128)S(1)}, u32[]{:S(2)}, u32[]{:S(2)}) async-start(f32[3,2,8,16]{3,1,0,2:T(2,128)} %copy.122), calls=%async_computation.7 | async-start | bytes 49152 | tf_op jit(solution)/shard_map/all_to_all | solution.py:145
  101.7 23.6 %all-to-all-start.2 = ((f32[3,2,2,128,128]{4,2,1,0,3:T(2,128)}), f32[3,2,2,128,128]{4,2,1,0,3:T(2,128)S(1)}, u32[]{:S(2)}, u32[]{:S(2)}) async-start(f32[3,2,2,128,128]{4,2,1,0,3:T(2,128)} %copy.100), calls=%async_computation.2 | async-start | bytes 1572864 | tf_op jit(solution)/shard_map/all_to_all | solution.py:137
  105.3 39.3 %collective-permute-start = (f32[4,1,64,128]{3,2,0,1:T(8,128)S(1)}, f32[4,1,64,128]{3,2,0,1:T(8,128)S(1)}, u32[]{:S(2)}, u32[]{:S(2)}) collective-permute-start(f32[4,1,64,128]{3,2,0,1:T(8,128)S(1)} %pad_maximum_fusion.11), channel_id=1, source_target_pairs={{0,2},{2,4},{4,6},{6,8},{8,10},{10,12},{12,14},{1,3},{3,5},{5,7},{... | collective-permute-start | bytes 393224 | tf_op jit(solution)/shard_map/ppermute | solution.py:29
  109.1 35.5 %collective-permute-start.1 = (f32[4,1,64,128]{3,2,0,1:T(8,128)S(1)}, f32[4,1,64,128]{3,2,0,1:T(8,128)S(1)}, u32[]{:S(2)}, u32[]{:S(2)}) collective-permute-start(f32[4,1,64,128]{3,2,0,1:T(8,128)S(1)} %pad_maximum_fusion.11), channel_id=1, source_target_pairs={{2,0},{4,2},{6,4},{8,6},{10,8},{12,10},{14,12},{3,1},{5,3},{7,5},{... | collective-permute-start | bytes 393224 | tf_op jit(solution)/shard_map/ppermute | solution.py:31
  128.3 19.8 %all-to-all-start.3 = ((f32[3,2,8,16,128]{4,3,0,1,2:T(8,128)}), f32[3,2,8,16,128]{4,3,0,1,2:T(8,128)S(1)}, u32[]{:S(2)}, u32[]{:S(2)}) async-start(f32[3,2,8,16,128]{4,3,0,1,2:T(8,128)} %copy.103), calls=%async_computation.3 | async-start | bytes 786432 | tf_op jit(solution)/shard_map/all_to_all | solution.py:144
  131.7 11.9 %reduce-scatter.4.cloned.1.call-start = ((), (), s32[]{:S(2)}) async-start(), calls=%async_computation.9 | async-start | bytes 98304
  134.1 38.2 %all-reduce.4.cloned.1.call-start = ((), (), s32[]{:S(2)}) async-start(), calls=%async_computation.10 | async-start | bytes 786432
  134.2 0.7 copy-start.5
  144.7 7.0 %collective-permute-start.2 = (f32[4,3,1,128]{3,2,0,1:T(1,128)S(1)}, f32[4,3,1,128]{3,2,0,1:T(1,128)S(1)}, u32[]{:S(2)}, u32[]{:S(2)}) collective-permute-start(f32[4,3,1,128]{3,2,0,1:T(1,128)S(1)} %get-tuple-element.19), channel_id=1, source_target_pairs={{0,1},{2,3},{4,5},{6,7},{8,9},{10,11},{12,13},{14,15},{16,17},{18,... | collective-permute-start | bytes 18440 | tf_op jit(solution)/shard_map/ppermute | solution.py:29
  146.8 4.9 %collective-permute-start.3 = (f32[4,3,1,128]{3,2,0,1:T(1,128)S(1)}, f32[4,3,1,128]{3,2,0,1:T(1,128)S(1)}, u32[]{:S(2)}, u32[]{:S(2)}) collective-permute-start(f32[4,3,1,128]{3,2,0,1:T(1,128)S(1)} %get-tuple-element.20), channel_id=1, source_target_pairs={{1,0},{3,2},{5,4},{7,6},{9,8},{11,10},{13,12},{15,14},{17,16},{19,... | collective-permute-start | bytes 18440 | tf_op jit(solution)/shard_map/ppermute | solution.py:31
Sparse Core Ops, SparseCore 0:
  134.7 8.8 reduce-scatter.3
  151.8 20.4 all-reduce.3
